TPU v7x, 32 devices: a 4x4x1 block of a 4x4x8 slice. The times are simulated.
32 devices in a mesh: batch: 1 (over z), py: 4 (over y), px: 8 (over x, core).
Axes of the slice: x: 4, y: 4, z: 1, core: 2. Of those that a mesh axis runs over, the one named last changes fastest.
The devices are a block of a 4x4x8 slice.
Arguments:
- pair_rep: bfloat16 [1024, 1024, 64], P(('batch', 'px'), 'py')
- pair_mask: int32 [1024, 1024], P(('batch', 'px'), 'py')
- ln_in: bfloat16 [2, 2, 64], replicated
- w_in: bfloat16 [2, 64, 320], replicated
- b_in: bfloat16 [2, 320], replicated
- ln_out: bfloat16 [2, 2, 64], replicated
- w_out: bfloat16 [2, 64, 64], replicated
- b_out: bfloat16 [2, 64], replicated
Outputs:
- output: bfloat16 [1024, 1024, 64], P(('batch', 'px'), 'py')
All inputs are finite; a program needn't handle non-finite values.
Results may differ from a plain program's by a relative error of at most 0.00639573.
Values are sent between devices in bfloat16 or wider.
A program may use at most 768 MiB of HBM per device.

v0:
```python
import jax
import jax.numpy as jnp
from jax import lax
from jax.sharding import PartitionSpec as P

LN_EPS = 1e-5


def layer_norm(values, ln_gain, ln_shift, norm_axis):
    average = jnp.mean(values, axis=norm_axis, keepdims=True)
    centered = values - average
    variance = jnp.mean(centered * centered, axis=norm_axis, keepdims=True)
    return centered * lax.rsqrt(variance + LN_EPS) * ln_gain + ln_shift


def gated_operands(pair_blk, mask_blk, ln_in, w_in, b_in):
    hidden = (w_in.shape[1] - w_in.shape[0]) // 4
    proj_width = 4 * hidden
    normed = layer_norm(pair_blk.astype(jnp.float32), ln_in[0].astype(jnp.float32), ln_in[1].astype(jnp.float32), -1).astype(jnp.bfloat16)
    projected = jnp.einsum('ijd,de->eij', normed, w_in[:, :proj_width], preferred_element_type=jnp.float32)
    projected = projected + b_in[:proj_width].astype(jnp.float32)[:, None, None]
    mask_f32 = mask_blk.astype(jnp.float32)[None]
    left_op = (mask_f32 * jax.nn.sigmoid(projected[:hidden]) * projected[hidden:2 * hidden]).astype(jnp.bfloat16)
    right_op = (mask_f32 * jax.nn.sigmoid(projected[2 * hidden:3 * hidden]) * projected[3 * hidden:]).astype(jnp.bfloat16)
    gate_val = jax.nn.sigmoid(jnp.einsum('ijd,de->ije', normed, w_in[:, proj_width:], preferred_element_type=jnp.float32) + b_in[proj_width:].astype(jnp.float32))
    return left_op, right_op, gate_val


def finish_update(pair_blk, tri_sum, gate_val, ln_out, w_out, b_out):
    normed_sum = layer_norm(tri_sum, ln_out[0].astype(jnp.float32)[:, None, None], ln_out[1].astype(jnp.float32)[:, None, None], 0).astype(jnp.bfloat16)
    update = jnp.einsum('cij,cd->ijd', normed_sum, w_out, preferred_element_type=jnp.float32) + b_out.astype(jnp.float32)
    return (pair_blk.astype(jnp.float32) + gate_val * update).astype(jnp.bfloat16)


def outgoing_sum(left_op, right_op):
    left_rows = lax.all_gather(left_op, 'py', axis=2, tiled=True)
    right_cols = lax.all_gather(right_op, 'px', axis=1, tiled=True)
    right_rows = lax.all_to_all(right_cols, 'py', 1, 2, tiled=True)
    return jnp.einsum('cik,cjk->cij', left_rows, right_rows, preferred_element_type=jnp.float32)


def incoming_sum(left_op, right_op):
    left_rows = lax.all_gather(left_op, 'py', axis=2, tiled=True)
    left_cols = lax.all_to_all(left_rows, 'px', 2, 1, tiled=True)
    right_cols = lax.all_gather(right_op, 'px', axis=1, tiled=True)
    return jnp.einsum('cki,ckj->cij', left_cols, right_cols, preferred_element_type=jnp.float32)


def solution(mesh):
    pair_spec = P(('batch', 'px'), 'py', None)
    mask_spec = P(('batch', 'px'), 'py')
    whole = P()

    def device_body(pair_blk, mask_blk, ln_in, w_in, b_in, ln_out, w_out, b_out):
        for update_idx in range(2):
            left_op, right_op, gate_val = gated_operands(pair_blk, mask_blk, ln_in[update_idx], w_in[update_idx], b_in[update_idx])
            if update_idx == 0:
                tri_sum = outgoing_sum(left_op, right_op)
            else:
                tri_sum = incoming_sum(left_op, right_op)
            pair_blk = finish_update(pair_blk, tri_sum, gate_val, ln_out[update_idx], w_out[update_idx], b_out[update_idx])
        return pair_blk

    return jax.shard_map(device_body, mesh=mesh, in_specs=(pair_spec, mask_spec, whole, whole, whole, whole, whole, whole), out_specs=pair_spec, check_vma=False)
```

profile of v0, /device:TPU:98, one launch (start us, length us, event | category | flops | bytes accessed | tf_op | source)
XLA Modules:
  0.0 1507.7 jit_solution(14870728550303476298)
XLA Ops:
  7.4 0.7 bitcast_convert_fusion.5
  8.2 3.5 convert_reduce_fusion.1
  11.7 4.0 fusion.12
  16.0 15.4 %add_bitcast_fusion.1 = f32[256,128,256]{2,0,1:T(8,128)} fusion(f32[256]{0:T(256)S(1)} %bitcast.90, bf16[64,320]{0,1:T(8,128)(2,1)S(1)} %bitcast.87, bf16[128,256,64]{1,2,0:T(8,128)(2,1)} %param.8, f32[64]{0:T(128)S(1)} %get-tuple-element.20, f32[64]{0:T(128)S(1)} %get-tuple-element.21, f32[128,256]{1,0:T(8,128)S(1)} %add_rsqrt_fusion.3, ...), kind=kOutput, calls=%fused_computation.4 | convolution fusion | flops 1094713344 | bytes 38078464 | tf_op jit(solution)/shard_map/ijd,de->eij/dot_general | solution.py:20
  31.4 16.3 %fusion.33 = (bf16[64,128,256]{2,0,1:T(8,128)(2,1)}, bf16[64,128,256]{2,0,1:T(8,128)(2,1)}) fusion(f32[256,128,256]{2,0,1:T(8,128)} %add_bitcast_fusion.1, f32[128,256]{1,0:T(8,128)S(1)} %convert_element_type.154), kind=kLoop, calls=%fused_computation.50 | loop fusion | flops 25165824 | bytes 42074112 | tf_op jit(solution)/shard_map/convert_element_type | solution.py:23
  47.8 157.3 %all-gather.7.cloned.1.call-done = bf16[64,1024,256]{2,0,1:T(8,128)(2,1)} async-done(((bf16[64,128,256]{2,0,1:T(8,128)(2,1)}), bf16[64,1024,256]{2,0,1:T(8,128)(2,1)}) %all-gather.7.cloned.1.call-update) | async-done | bytes 33554448 | tf_op jit(solution)/shard_map/all_gather | solution.py:37
  205.1 9.8 all-to-all-start
  215.0 0.6 all-gather.5.cloned.1.call-update
  216.5 0.6 bitcast_convert_fusion
  217.1 496.6 %all-to-all-done = bf16[64,1024,256]{2,0,1:T(8,128)(2,1)} async-done(((bf16[64,1024,256]{2,0,1:T(8,128)(2,1)}), bf16[64,1024,256]{2,0,1:T(8,128)(2,1)}, u32[]{:S(2)}, u32[]{:S(2)}) %all-to-all-start) | async-done | bytes 33554464 | tf_op jit(solution)/shard_map/all_to_all | solution.py:38
  713.7 42.4 %copy.69 = bf16[64,4,256,256]{3,1,2,0:T(4,128)(2,1)} copy(bf16[64,4,256,256]{3,0,2,1:T(8,128)(2,1)} %bitcast.8) | data formatting | bytes 67108864 | tf_op jit(solution)/shard_map/all_to_all | solution.py:38
  756.1 53.6 %all_to_all.29 = bf16[64,256,1024]{2,1,0:T(8,128)(2,1)} reshape(bf16[64,256,4,256]{3,2,1,0:T(4,128)(2,1)} %bitcast.82) | data formatting | bytes 67108864 | tf_op jit(solution)/shard_map/all_to_all | solution.py:38
  809.6 26.6 %fusion.51 = (f32[128,256]{1,0:T(8,128)S(1)}, f32[64,128,256]{2,1,0:T(8,128)}) fusion(bf16[64,256,1024]{2,1,0:T(8,128)(2,1)} %all_to_all.29, bf16[64,128,1024]{2,0,1:T(8,128)(2,1)} %all-gather.5.cloned.1.call-done), kind=kOutput, calls=%fused_computation.95 | convolution fusion | flops 4297031680 | bytes 58851328 | tf_op jit(solution)/shard_map/cik,cjk->cij/dot_general | solution.py:39
  836.3 4.4 multiply_reduce_fusion.1
  840.7 1.3 copy-done.2
  842.0 2.0 add_convert_fusion.1
  844.1 3.3 fusion.40
  847.4 5.9 convert_reduce_fusion
  853.3 2.0 fusion.8
  855.3 13.4 add_bitcast_fusion
  868.6 16.3 %fusion.18 = (bf16[64,128,256]{2,0,1:T(8,128)(2,1)}, bf16[64,128,256]{2,0,1:T(8,128)(2,1)}) fusion(f32[256,128,256]{2,0,1:T(8,128)} %add_bitcast_fusion, f32[128,256]{1,0:T(8,128)S(1)} %convert_element_type.154), kind=kLoop, calls=%fused_computation.29 | loop fusion | flops 25165824 | bytes 42074112 | tf_op jit(solution)/shard_map/convert_element_type | solution.py:24
  885.6 154.2 %all-gather.9.cloned.1.call-done = bf16[64,128,1024]{2,0,1:T(8,128)(2,1)} async-done(((bf16[64,128,256]{2,0,1:T(8,128)(2,1)}), bf16[64,128,1024]{2,0,1:T(8,128)(2,1)}) %all-gather.9.cloned.1.call-update) | async-done | bytes 16777232 | tf_op jit(solution)/shard_map/all_gather | solution.py:43
  1039.8 25.9 %copy.42 = bf16[64,128,1024]{1,0,2:T(8,128)(2,1)} copy(bf16[64,128,1024]{2,0,1:T(8,128)(2,1)} %all-gather.9.cloned.1.call-done) | data formatting | bytes 33554432 | tf_op jit(solution)/shard_map/all_gather | solution.py:43
  1065.7 308.5 %all_to_all.36 = bf16[64,128,1024]{1,0,2:T(8,128)(2,1)S(1)} all-to-all(bf16[64,128,1024]{1,0,2:T(8,128)(2,1)} %copy.42), channel_id=1, replica_groups=mesh['batch'=1,'py'=4,'px'=8] {'px'}, dimensions={2} | all-to-all | bytes 33554432 | tf_op jit(solution)/shard_map/all_to_all | solution.py:44
  1374.2 36.0 %copy.70 = bf16[64,128,8,128]{1,2,3,0:T(8,128)(2,1)} copy(bf16[64,128,8,128]{1,0,3,2:T(8,128)(2,1)S(1)} %bitcast.83) | data formatting | bytes 33554432 | tf_op jit(solution)/shard_map/all_to_all | solution.py:44
  1410.2 25.3 %all_to_all.33 = bf16[64,1024,128]{1,2,0:T(8,128)(2,1)} reshape(bf16[64,8,128,128]{2,1,3,0:T(8,128)(2,1)} %bitcast.84) | data formatting | bytes 33554432 | tf_op jit(solution)/shard_map/all_to_all | solution.py:44
  1435.5 46.5 %fusion.52 = (f32[128,256]{1,0:T(8,128)S(1)}, f32[64,128,256]{2,1,0:T(8,128)}) fusion(bf16[64,1024,128]{1,2,0:T(8,128)(2,1)} %all_to_all.33, bf16[64,1024,256]{2,0,1:T(8,128)(2,1)} %all-gather.11.cloned.1.call-done), kind=kOutput, calls=%fused_computation.96 | convolution fusion | flops 4297031680 | bytes 58851328 | tf_op jit(solution)/shard_map/cki,ckj->cij/dot_general | solution.py:46
  1482.1 4.4 multiply_reduce_fusion
  1486.5 1.3 copy-done.1
  1487.8 2.3 add_convert_fusion
  1490.1 3.3 fusion.38
  1493.4 6.4 fusion.17
  (51 shorter events, 2.1 us)
Async XLA Ops:
  7.4 8.4 copy-start.6
  7.4 8.5 copy-start.8
  7.4 8.5 copy-start.5
  7.4 197.7 %all-gather.7.cloned.1.call-start = ((), (), s32[]{:S(2)}) async-start(), calls=%async_computation.3 | async-start | bytes 37748736 | tf_op jit(solution)/shard_map/all_gather | solution.py:37
  47.8 168.2 %copy-start.9 = (bf16[2,2,64]{2,1,0:T(2,128)(2,1)S(1)}, bf16[2,2,64]{2,1,0:T(2,128)(2,1)}, u32[]{:S(2)}) copy-start(bf16[2,2,64]{2,1,0:T(2,128)(2,1)} %param.13) | copy-start | bytes 1540
  47.8 168.7 %copy-start.12 = (bf16[2,64]{1,0:T(2,128)(2,1)S(1)}, bf16[2,64]{1,0:T(2,128)(2,1)}, u32[]{:S(2)}) copy-start(bf16[2,64]{1,0:T(2,128)(2,1)} %param.15) | copy-start | bytes 772
  205.1 508.6 %all-to-all-start = ((bf16[64,1024,256]{2,0,1:T(8,128)(2,1)}), bf16[64,1024,256]{2,0,1:T(8,128)(2,1)}, u32[]{:S(2)}, u32[]{:S(2)}) async-start(bf16[64,1024,256]{2,0,1:T(8,128)(2,1)} %all-gather.7.cloned.1.call-done), calls=%async_computation | async-start | bytes 67108864 | tf_op jit(solution)/shard_map/all_to_all | solution.py:38
  214.9 594.7 %all-gather.5.cloned.1.call-start = ((), (), s32[]{:S(2)}) async-start(), calls=%async_computation.2 | async-start | bytes 20971520 | tf_op jit(solution)/shard_map/all_gather | solution.py:36
  215.5 824.3 %all-gather.9.cloned.1.call-start = ((), (), s32[]{:S(2)}) async-start(), calls=%async_computation.4 | async-start | bytes 20971520 | tf_op jit(solution)/shard_map/all_gather | solution.py:43
  836.2 5.8 copy-start.2
  840.6 3.4 copy-start.7
  844.1 3.3 copy-start
  853.2 15.4 %copy-start.3 = (bf16[128,256,64]{1,2,0:T(8,128)(2,1)}, bf16[128,256,64]{1,2,0:T(8,128)(2,1)S(1)}, u32[]{:S(2)}) copy-start(bf16[128,256,64]{1,2,0:T(8,128)(2,1)S(1)} %get-tuple-element.28) | copy-start | bytes 12582916
  885.0 550.5 %all-gather.11.cloned.1.call-start = ((), (), s32[]{:S(2)}) async-start(), calls=%async_computation.5 | async-start | bytes 37748736 | tf_op jit(solution)/shard_map/all_gather | solution.py:45
  1482.0 5.8 copy-start.1
  1482.0 5.8 copy-start.10
  1482.1 5.8 copy-start.11
  1490.1 3.3 copy-start.4
  1490.1 3.3 copy-start.13
  1490.1 3.3 copy-start.14
Sparse Core Ops, SparseCore 0:
  47.9 157.1 all-gather.6
Sparse Core Ops, SparseCore 1:
  217.0 294.0 all-gather.4
  885.1 154.7 all-gather.8
  1041.3 333.1 all-gather.10
where the time goes:
time: 1520 us; the launch traced here: 1510 us
  waiting for transfers between devices  809 us (53%)
  blocking collectives  309 us (20%)
  local copies, waits for them, and re-layouts  186 us (12%)
  matrix products  121 us (8%)
  other arithmetic  57.2 us (4%)
  between operations  15.6 us (1%)
    all_to_all x1, waiting for transfers between devices, outgoing_sum(): right_rows = lax.all_to_all(right_cols, 'py', 1, 2, tiled=True)  497 us
    all_to_all x1, blocking collectives, incoming_sum(): left_cols = lax.all_to_all(left_rows, 'px', 2, 1, tiled=True)  309 us
    all_gather x1, waiting for transfers between devices, outgoing_sum(): right_cols = lax.all_gather(right_op, 'px', axis=1, tiled=True)  157 us
    all_gather x1, waiting for transfers between devices, incoming_sum(): left_rows = lax.all_gather(left_op, 'py', axis=2, tiled=True)  154 us
    all_to_all x2, local copies, waits for them, and re-layouts, outgoing_sum(): right_rows = lax.all_to_all(right_cols, 'py', 1, 2, tiled=True)  95.9 us
    all_to_all x2, local copies, waits for them, and re-layouts, incoming_sum(): left_cols = lax.all_to_all(left_rows, 'px', 2, 1, tiled=True)  61.3 us
    dot_general x1, matrix products, incoming_sum(): jnp.einsum('cki,ckj->cij', left_cols, right_cols, preferred_element_type=...  46.5 us
  transfers between devices with their start and end apart: 5, of which 3 were waited for; matrix products, arithmetic and copies ran while one was open for 7% of the time, Pallas kernels for 0%

commit v1 on v0

v1 whole, which is shorter than its diff:
```python
import functools

import jax
import jax.numpy as jnp
from jax import lax
from jax.experimental import pallas as pl
from jax.experimental.pallas import tpu as pltpu
from jax.sharding import PartitionSpec as P

LN_EPS = 1e-5
SUB = 8
GATE_ROWS = 4
MESH = pl.DeviceIdType.MESH
BF16 = jnp.bfloat16
F32 = jnp.float32


def dot(lhs, rhs, dims=((1,), (0,))):
    return lax.dot_general(lhs, rhs, (dims, ((), ())), preferred_element_type=F32)


def tree_sum(parts):
    while len(parts) > 1:
        parts = [parts[k] + parts[k + 1] if k + 1 < len(parts) else parts[k] for k in range(0, len(parts), 2)]
    return parts[0]


def kernel(npy, npx, z_ref, mask_ref, wab_ref, bab_ref, ln_in_ref, wg_ref, bg_ref, ln_out_ref, wo_ref, bo_ref,
           out_ref, zn, proj, xn, ab_out, ab_in, a_t, x_out, x_in,
           ab_ss, ab_rs, x_ss, x_rs, free_sem):
    rows, dim, cols = z_ref.shape
    hidden = x_in.shape[0]
    n = npy * npx
    slots = hidden // n
    full = npx * rows
    tile = 2 * rows
    my_py, my_px = lax.axis_index('py'), lax.axis_index('px')
    my_x, my_core = my_px // 2, lax.rem(my_px, 2)
    nx = npx // 2

    def peer(off):
        f, t, e = off
        dpy = lax.rem(my_py + f, npy)
        dpx = 2 * lax.rem(my_x + t, nx) + lax.rem(my_core + e, 2)
        return dpy, dpx

    def lin(dev):
        return dev[0] * npx + dev[1]

    def dev_id(dev):
        return {'py': dev[0], 'px': dev[1]}

    me = (my_py, my_px)
    here = lin(me)
    offsets = [((s + s // nx) % npy, s % nx, e) for s in range(npy * nx) for e in range(2)]
    others = [o for o in offsets if o != (0, 0, 0)]

    def at_rows(dev):
        return pl.ds(pl.multiple_of(dev[1] * rows, rows), rows)

    def at_cols(dev):
        return pl.ds(pl.multiple_of(dev[0] * cols, cols), cols)

    def ab_copy(s, src, dst):
        return pltpu.make_async_remote_copy(
            src_ref=ab_out.at[s, lin(dst)], dst_ref=ab_in.at[s, :, at_rows(src), at_cols(src)],
            send_sem=ab_ss.at[s, lin(dst)], recv_sem=ab_rs.at[s, lin(src)],
            device_id=dev_id(dst), device_id_type=MESH)

    def x_copy(s, src, dst):
        return pltpu.make_async_remote_copy(
            src_ref=x_out.at[s, at_rows(dst), at_cols(dst)], dst_ref=x_in.at[s * n + lin(src)],
            send_sem=x_ss.at[s, lin(dst)], recv_sem=x_rs.at[s, lin(src)],
            device_id=dev_id(dst), device_id_type=MESH)

    def normalize(src_ref, u):
        gain, shift = ln_in_ref[u, 0], ln_in_ref[u, 1]

        @pl.loop(0, rows)
        def _(i):
            for h in range(cols // 128):
                lanes = pl.ds(h * 128, 128)
                val = src_ref[i, :, lanes].astype(F32)
                cen = val - jnp.mean(val, axis=0, keepdims=True)
                var = jnp.mean(cen * cen, axis=0, keepdims=True)
                zn[i, :, lanes] = (cen * lax.rsqrt(var + LN_EPS) * gain + shift).astype(BF16)

    def project(u, s):
        @pl.loop(0, rows // (2 * SUB))
        def _(g):
            for h in range(2):
                rhs = zn[pl.ds(g * 2 * SUB + h * SUB, SUB)].reshape(SUB * dim, cols)
                proj[h, pl.ds(0, 4 * n * SUB), :] = dot(wab_ref[u, s], rhs)
            at = pl.ds(pl.multiple_of(g * 2 * SUB, 2 * SUB), 2 * SUB)
            mask = mask_ref[at, :].astype(F32)

            @pl.loop(0, n, unroll=2)
            def _(d):
                for op in range(2):
                    bias_g, bias_p = bab_ref[u, s, 2 * op, d], bab_ref[u, s, 2 * op + 1, d]
                    g_at = pl.ds(pl.multiple_of((2 * op * n + d) * SUB, SUB), SUB)
                    p_at = pl.ds(pl.multiple_of(((2 * op + 1) * n + d) * SUB, SUB), SUB)
                    gate = jnp.concatenate([proj[0, g_at, :], proj[1, g_at, :]], axis=0) + bias_g
                    lin_p = jnp.concatenate([proj[0, p_at, :], proj[1, p_at, :]], axis=0) + bias_p
                    ab_out[s, d, op, at, :] = (mask * jax.nn.sigmoid(gate) * lin_p).astype(BF16)

    def send_ab(s):
        for off in others:
            ab_copy(s, me, peer(off)).start()
        ab_in[s, :, at_rows(me), at_cols(me)] = ab_out[s, here]

    def products(u, s):
        for t in range(nx):
            m = lax.rem(my_x + t, nx)
            m_at = pl.ds(pl.multiple_of(m * tile, tile), tile)
            if u == 0:
                lhs_ref = ab_in.at[s, 0, m_at, :]
            else:
                a_t[...] = ab_in[s, 0, :, m_at].T
                lhs_ref = a_t

            @pl.loop(0, full // cols)
            def _(q):
                q_at = pl.ds(pl.multiple_of(q * cols, cols), cols)
                if u == 0:
                    x_out[s, m_at, q_at] = dot(lhs_ref[...], ab_in[s, 1, q_at, :], ((1,), (1,)))
                else:
                    x_out[s, m_at, q_at] = dot(lhs_ref[...], ab_in[s, 1, :, q_at])

            for off in offsets:
                if off[1] == t:
                    if off == (0, 0, 0):
                        x_in[s * n + here] = x_out[s, at_rows(me), at_cols(me)]
                    else:
                        x_copy(s, me, peer(off)).start()

    def finish(src_ref, u):
        @pl.loop(0, rows // SUB)
        def _(g):
            at = pl.ds(pl.multiple_of(g * SUB, SUB), SUB)
            for h in range(cols // 128):
                lanes = pl.ds(h * 128, 128)
                avg = tree_sum([x_in[c, at, lanes] for c in range(hidden)]) * (1.0 / hidden)
                var = tree_sum([jnp.square(x_in[c, at, lanes] - avg) for c in range(hidden)]) * (1.0 / hidden)
                inv = lax.rsqrt(var + LN_EPS)
                for c in range(0, hidden, 2):
                    pair = [(x_in[k, at, lanes] - avg) * inv * ln_out_ref[u, 0, k] + ln_out_ref[u, 1, k] for k in (c, c + 1)]
                    xn[pl.ds(c * SUB, 2 * SUB), lanes] = jnp.concatenate(pair, axis=0).astype(BF16)
            proj[0, pl.ds(0, SUB * dim), :] = dot(wo_ref[u], xn[...])
            for k in range(SUB // GATE_ROWS):
                rhs = zn[pl.ds(g * SUB + k * GATE_ROWS, GATE_ROWS)].reshape(GATE_ROWS * dim, cols)
                proj[1, pl.ds(k * GATE_ROWS * dim, GATE_ROWS * dim), :] = dot(wg_ref[u], rhs)

            @pl.loop(0, SUB)
            def _(r):
                r_at = pl.ds(pl.multiple_of(r * dim, dim), dim)
                for h in range(cols // 128):
                    lanes = pl.ds(h * 128, 128)
                    gate = jax.nn.sigmoid(proj[1, r_at, lanes] + bg_ref[u])
                    upd = proj[0, r_at, lanes] + bo_ref[u]
                    out_ref[g * SUB + r, :, lanes] = (src_ref[g * SUB + r, :, lanes].astype(F32) + gate * upd).astype(BF16)

    barrier = pltpu.get_barrier_semaphore()
    for off in others:
        pl.semaphore_signal(barrier, inc=1, device_id=dev_id(peer(off)), device_id_type=MESH)
    normalize(z_ref, 0)
    pl.semaphore_wait(barrier, n - 1)

    for u in range(2):
        src_ref = z_ref if u == 0 else out_ref
        if u == 1:
            normalize(src_ref, u)
            for s in range(slots):
                for off in others:
                    ab_copy(s, me, peer(off)).wait_send()
            pl.semaphore_wait(free_sem, n - 1)
        for s in range(slots):
            project(u, s)
            send_ab(s)
        for s in range(slots):
            for off in others:
                ab_copy(s, peer(off), me).wait_recv()
            if u == 1:
                for off in others:
                    x_copy(s, me, peer(off)).wait_send()
            products(u, s)
        if u == 0:
            for off in others:
                pl.semaphore_signal(free_sem, inc=1, device_id=dev_id(peer(off)), device_id_type=MESH)
        for s in range(slots):
            for off in others:
                x_copy(s, peer(off), me).wait_recv()
        finish(src_ref, u)
    for s in range(slots):
        for off in others:
            ab_copy(s, me, peer(off)).wait_send()
            x_copy(s, me, peer(off)).wait_send()


def solution(mesh):
    pair_spec = P(('batch', 'px'), 'py', None)
    mask_spec = P(('batch', 'px'), 'py')
    whole = P()
    npy, npx = mesh.shape['py'], mesh.shape['px']
    n = npy * npx

    def device_body(pair_blk, mask_blk, ln_in, w_in, b_in, ln_out, w_out, b_out):
        rows, cols, dim = pair_blk.shape
        hidden = w_out.shape[1]
        slots = hidden // n
        full = npx * rows
        updates = w_in.shape[0]
        zero = jnp.zeros((), BF16)
        eye8 = jnp.eye(SUB, dtype=jnp.bool_)
        eye4 = jnp.eye(GATE_ROWS, dtype=jnp.bool_)

        w_t = jnp.swapaxes(w_in, 1, 2)
        wab = w_t[:, :4 * hidden].reshape(updates, 4, slots, n, dim).transpose(0, 2, 1, 3, 4)
        wab = wab.reshape(updates, slots, 4 * n, 1, 1, dim)
        wab = jnp.where(eye8[:, :, None], wab, zero).reshape(updates, slots, 4 * n * SUB, SUB * dim)
        bab = b_in[:, :4 * hidden].astype(F32).reshape(updates, 4, slots, n).transpose(0, 2, 1, 3)
        wg = w_t[:, 4 * hidden:].reshape(updates, 1, dim, 1, dim)
        wg = jnp.where(eye4[:, None, :, None], wg, zero).reshape(updates, GATE_ROWS * dim, GATE_ROWS * dim)
        wo = jnp.swapaxes(w_out, 1, 2).reshape(updates, 1, dim, hidden, 1)
        wo = jnp.where(eye8[:, None, None, :], wo, zero).reshape(updates, SUB * dim, SUB * hidden)
        bg = jnp.broadcast_to(b_in[:, 4 * hidden:, None].astype(F32), (updates, dim, 128))
        bo = jnp.broadcast_to(b_out[:, :, None].astype(F32), (updates, dim, 128))
        ln_i = jnp.broadcast_to(ln_in[:, :, :, None].astype(F32), (updates, 2, dim, 128))
        ln_o = jnp.broadcast_to(ln_out[:, :, :, None, None].astype(F32), (updates, 2, hidden, SUB, 128))

        vmem = pl.BlockSpec(memory_space=pltpu.VMEM)
        smem = pl.BlockSpec(memory_space=pltpu.SMEM)
        out = pl.pallas_call(
            functools.partial(kernel, npy, npx),
            out_shape=jax.ShapeDtypeStruct((rows, dim, cols), BF16),
            in_specs=[vmem, vmem, vmem, smem] + [vmem] * 6,
            out_specs=vmem,
            scratch_shapes=[
                pltpu.VMEM((rows, dim, cols), BF16),
                pltpu.VMEM((2, SUB * max(4 * n, dim), cols), F32),
                pltpu.VMEM((SUB * hidden, cols), BF16),
                pltpu.VMEM((slots, n, 2, rows, cols), BF16),
                pltpu.VMEM((slots, 2, full, full), BF16),
                pltpu.VMEM((2 * rows, full), BF16),
                pltpu.VMEM((slots, full, full), F32),
                pltpu.VMEM((hidden, rows, cols), F32),
                pltpu.SemaphoreType.DMA((slots, n)),
                pltpu.SemaphoreType.DMA((slots, n)),
                pltpu.SemaphoreType.DMA((slots, n)),
                pltpu.SemaphoreType.DMA((slots, n)),
                pltpu.SemaphoreType.REGULAR,
            ],
            compiler_params=pltpu.CompilerParams(collective_id=0, has_side_effects=True, vmem_limit_bytes=67043328),
            name='triangle',
        )(jnp.swapaxes(pair_blk, 1, 2), mask_blk, wab, bab, ln_i, wg, bg, ln_o, wo, bo)
        return jnp.swapaxes(out, 1, 2)

    return jax.shard_map(device_body, mesh=mesh, in_specs=(pair_spec, mask_spec, whole, whole, whole, whole, whole, whole), out_specs=pair_spec, check_vma=False)
```

time: 1520 us -> 571 us (0.38)
  the two profiles are of different devices: /device:TPU:98 before, /device:TPU:104 now
where the time goes in v1:
time: 571 us; the launch traced here: 570 us
  Pallas kernels  530 us (93%)
  local copies, waits for them, and re-layouts  33 us (6%)
  other arithmetic  6.96 us (1%)
    pallas_call x1, Pallas kernels, device_body(): pl.pallas_call(functools.partial(kernel, npy, npx), out_shape=jax.ShapeDt...  530 us
    broadcast_in_dim x4, local copies, waits for them, and re-layouts, device_body(): jnp.where(eye8[:, :, None], wab, zero)  17.8 us

profile of v1, /device:TPU:104, one launch (start us, length us, event | category | flops | bytes accessed | tf_op | source)
XLA Modules:
  0.0 570.3 jit_solution(3767034306956514661)
XLA Ops:
  0.0 1.1 copy.12
  1.1 4.3 broadcast_in_dim.111
  5.4 11.8 %broadcast_in_dim.112 = bf16[2,2,1024,512]{3,2,1,0:T(8,128)(2,1)} reshape(bf16[2,2,128,8,8,64]{5,4,3,2,1,0:T(8,128)(2,1)} %broadcast_in_dim.111) | data formatting | bytes 8388608 | tf_op jit(solution)/shard_map/jit(_where)/broadcast_in_dim | solution.py:220
  17.2 0.1 copy.11
  17.3 0.3 broadcast_in_dim.107
  17.6 1.4 broadcast_in_dim.108
  19.1 0.0 copy-start.1
  19.1 5.1 broadcast_select_fusion.wab_ref
  24.2 0.2 broadcast_in_dim.123
  24.4 0.7 broadcast_in_dim.124
  25.1 0.4 copy.15
  25.5 0.3 broadcast_in_dim.126
  25.8 0.0 copy-start.2
  25.8 1.3 broadcast_in_dim.127
  27.0 0.0 copy-start.3
  27.1 0.0 copy-start.5
  27.1 0.5 copy.16
  27.6 1.1 broadcast_select_fusion.1.wo_ref
  28.7 0.8 slice.17
  29.5 0.1 broadcast_in_dim.118
  29.6 0.3 broadcast_in_dim.119
  30.0 0.1 broadcast_in_dim.115
  30.1 0.2 broadcast_in_dim.116
  30.4 0.7 broadcast_select_fusion.2.wg_ref
  31.1 1.3 broadcast_in_dim.122.ln_out_ref
  32.5 0.7 broadcast_in_dim.114.ln_in_ref
  33.2 0.7 broadcast_in_dim.121.bg_ref
  33.9 0.7 broadcast_in_dim.129.bo_ref
  34.6 0.1 reshape.32
  34.7 0.6 copy.18
  35.3 530.1 %triangle.1 = bf16[128,64,256]{2,1,0:T(8,128)(2,1)} custom-call(bf16[128,64,256]{2,1,0:T(8,128)(2,1)} %bitcast.24, s32[128,256]{1,0:T(8,128)} %mask_ref.1, bf16[2,2,1024,512]{3,2,1,0:T(8,128)(2,1)} %broadcast_select_fusion.wab_ref, f32[2,2,4,32]{3,2,1,0:T(4,128)} %bitcast.29, f32[2,2,64,128]{3,2,1,0:T(8,128)} %broadcast_in_dim.114.ln_in_ref, ...), custom_call_target="tpu_custom_call" | custom-call | tf_op jit(solution)/shard_map/triangle/pallas_call | solution.py:233
  565.5 4.8 copy.20
  (14 shorter events, 0.1 us)
Async XLA Ops:
  1.1 4.4 copy-start
  19.1 6.4 %copy-start.1 = (bf16[2,64,64]{2,1,0:T(8,128)(2,1)S(1)}, bf16[2,64,64]{2,1,0:T(8,128)(2,1)}, u32[]{:S(2)}) copy-start(bf16[2,64,64]{2,1,0:T(8,128)(2,1)} %param.14) | copy-start | bytes 49156
  25.8 5.4 copy-start.2
  27.0 5.4 copy-start.3
  27.1 6.2 %copy-start.4 = (bf16[2,320]{1,0:T(2,128)(2,1)S(1)}, bf16[2,320]{1,0:T(2,128)(2,1)}, u32[]{:S(2)}) copy-start(bf16[2,320]{1,0:T(2,128)(2,1)} %param.12) | copy-start | bytes 3844
  27.1 6.9 %copy-start.5 = (bf16[2,64]{1,0:T(2,128)(2,1)S(1)}, bf16[2,64]{1,0:T(2,128)(2,1)}, u32[]{:S(2)}) copy-start(bf16[2,64]{1,0:T(2,128)(2,1)} %param.15) | copy-start | bytes 772

commit v2 on v1

--- a/solution.py
+++ b/solution.py
@@ -25,11 +25,12 @@
     return parts[0]
 
 
-def kernel(npy, npx, z_ref, mask_ref, wab_ref, bab_ref, ln_in_ref, wg_ref, bg_ref, ln_out_ref, wo_ref, bo_ref,
-           out_ref, zn, proj, xn, ab_out, ab_in, a_t, x_out, x_in,
+def kernel(npy, npx, z_ref, mask_ref, w_in_ref, w_out_ref, bias_ref, vec_ref,
+           out_ref, w_t, wab, wg, wo, zn, proj, xn, ab_out, ab_in, a_t, x_out, x_in,
            ab_ss, ab_rs, x_ss, x_rs, free_sem):
     rows, dim, cols = z_ref.shape
     hidden = x_in.shape[0]
+    width = w_in_ref.shape[2]
     n = npy * npx
     slots = hidden // n
     full = npx * rows
@@ -52,8 +53,13 @@
 
     me = (my_py, my_px)
     here = lin(me)
-    offsets = [((s + s // nx) % npy, s % nx, e) for s in range(npy * nx) for e in range(2)]
-    others = [o for o in offsets if o != (0, 0, 0)]
+    def reach(off):
+        hops = [min(off[0], npy - off[0]), min(off[1], nx - off[1])]
+        halfway = 2 * off[0] == npy or 2 * off[1] == nx
+        return halfway, sum(hops)
+
+    diagonal = [((k + k // nx) % npy, k % nx, e) for k in range(npy * nx) for e in range(2)]
+    others = sorted([off for off in diagonal if off != (0, 0, 0)], key=reach)
 
     def at_rows(dev):
         return pl.ds(pl.multiple_of(dev[1] * rows, rows), rows)
@@ -73,8 +79,34 @@
             send_sem=x_ss.at[s, lin(dst)], recv_sem=x_rs.at[s, lin(src)],
             device_id=dev_id(dst), device_id_type=MESH)
 
+    def iota(shape, axis):
+        return lax.broadcasted_iota(jnp.int32, shape, axis)
+
+    def spread_weights(u):
+        wide = (dim, SUB * dim)
+        pick = (lax.rem(iota(wide, 1), dim) == iota(wide, 0)).astype(F32).astype(BF16)
+        w_t[...] = dot(w_in_ref[u], pick, ((0,), (0,))).astype(BF16)
+        big = (n * SUB, SUB * dim)
+        keep = lax.rem(iota(big, 0), SUB) == iota(big, 1) // dim
+        sel = (n * SUB, width)
+        for s in range(slots):
+            for k in range(4):
+                first = k * hidden + s * n
+                rep = (iota(sel, 0) // SUB + first == iota(sel, 1)).astype(F32).astype(BF16)
+                wab[s, pl.ds(k * n * SUB, n * SUB), :] = jnp.where(keep, dot(rep, w_t[...]), 0.0).astype(BF16)
+        gate_w = w_t[pl.ds(4 * hidden, dim), pl.ds(0, GATE_ROWS * dim)].astype(F32)
+        lane = iota(gate_w.shape, 1)
+        for r in range(GATE_ROWS):
+            wg[pl.ds(r * dim, dim), :] = jnp.where(lane // dim == r, gate_w, 0.0).astype(BF16)
+        wide = (hidden, SUB * hidden)
+        pick = (iota(wide, 1) // SUB == iota(wide, 0)).astype(F32).astype(BF16)
+        out_w = dot(w_out_ref[u], pick, ((0,), (0,)))
+        lane = iota(out_w.shape, 1)
+        for r in range(SUB):
+            wo[pl.ds(r * dim, dim), :] = jnp.where(lax.rem(lane, SUB) == r, out_w, 0.0).astype(BF16)
+
     def normalize(src_ref, u):
-        gain, shift = ln_in_ref[u, 0], ln_in_ref[u, 1]
+        gain, shift = vec_ref[u, 0], vec_ref[u, 1]
 
         @pl.loop(0, rows)
         def _(i):
@@ -90,14 +122,14 @@
         def _(g):
             for h in range(2):
                 rhs = zn[pl.ds(g * 2 * SUB + h * SUB, SUB)].reshape(SUB * dim, cols)
-                proj[h, pl.ds(0, 4 * n * SUB), :] = dot(wab_ref[u, s], rhs)
+                proj[h, pl.ds(0, 4 * n * SUB), :] = dot(wab[s], rhs)
             at = pl.ds(pl.multiple_of(g * 2 * SUB, 2 * SUB), 2 * SUB)
             mask = mask_ref[at, :].astype(F32)
 
             @pl.loop(0, n, unroll=2)
             def _(d):
                 for op in range(2):
-                    bias_g, bias_p = bab_ref[u, s, 2 * op, d], bab_ref[u, s, 2 * op + 1, d]
+                    bias_g, bias_p = bias_ref[u, 2 * op * hidden + s * n + d], bias_ref[u, (2 * op + 1) * hidden + s * n + d]
                     g_at = pl.ds(pl.multiple_of((2 * op * n + d) * SUB, SUB), SUB)
                     p_at = pl.ds(pl.multiple_of(((2 * op + 1) * n + d) * SUB, SUB), SUB)
                     gate = jnp.concatenate([proj[0, g_at, :], proj[1, g_at, :]], axis=0) + bias_g
@@ -127,12 +159,9 @@
                 else:
                     x_out[s, m_at, q_at] = dot(lhs_ref[...], ab_in[s, 1, :, q_at])
 
-            for off in offsets:
-                if off[1] == t:
-                    if off == (0, 0, 0):
-                        x_in[s * n + here] = x_out[s, at_rows(me), at_cols(me)]
-                    else:
-                        x_copy(s, me, peer(off)).start()
+        for off in others:
+            x_copy(s, me, peer(off)).start()
+        x_in[s * n + here] = x_out[s, at_rows(me), at_cols(me)]
 
     def finish(src_ref, u):
         @pl.loop(0, rows // SUB)
@@ -144,31 +173,33 @@
                 var = tree_sum([jnp.square(x_in[c, at, lanes] - avg) for c in range(hidden)]) * (1.0 / hidden)
                 inv = lax.rsqrt(var + LN_EPS)
                 for c in range(0, hidden, 2):
-                    pair = [(x_in[k, at, lanes] - avg) * inv * ln_out_ref[u, 0, k] + ln_out_ref[u, 1, k] for k in (c, c + 1)]
+                    pair = [(x_in[k, at, lanes] - avg) * inv * vec_ref[u, 4, pl.ds(k, 1), :] + vec_ref[u, 5, pl.ds(k, 1), :] for k in (c, c + 1)]
                     xn[pl.ds(c * SUB, 2 * SUB), lanes] = jnp.concatenate(pair, axis=0).astype(BF16)
-            proj[0, pl.ds(0, SUB * dim), :] = dot(wo_ref[u], xn[...])
+            proj[0, pl.ds(0, SUB * dim), :] = dot(wo[...], xn[...])
             for k in range(SUB // GATE_ROWS):
                 rhs = zn[pl.ds(g * SUB + k * GATE_ROWS, GATE_ROWS)].reshape(GATE_ROWS * dim, cols)
-                proj[1, pl.ds(k * GATE_ROWS * dim, GATE_ROWS * dim), :] = dot(wg_ref[u], rhs)
+                proj[1, pl.ds(k * GATE_ROWS * dim, GATE_ROWS * dim), :] = dot(wg[...], rhs)
 
             @pl.loop(0, SUB)
             def _(r):
                 r_at = pl.ds(pl.multiple_of(r * dim, dim), dim)
                 for h in range(cols // 128):
                     lanes = pl.ds(h * 128, 128)
-                    gate = jax.nn.sigmoid(proj[1, r_at, lanes] + bg_ref[u])
-                    upd = proj[0, r_at, lanes] + bo_ref[u]
+                    gate = jax.nn.sigmoid(proj[1, r_at, lanes] + vec_ref[u, 2])
+                    upd = proj[0, r_at, lanes] + vec_ref[u, 3]
                     out_ref[g * SUB + r, :, lanes] = (src_ref[g * SUB + r, :, lanes].astype(F32) + gate * upd).astype(BF16)
 
     barrier = pltpu.get_barrier_semaphore()
     for off in others:
         pl.semaphore_signal(barrier, inc=1, device_id=dev_id(peer(off)), device_id_type=MESH)
+    spread_weights(0)
     normalize(z_ref, 0)
     pl.semaphore_wait(barrier, n - 1)
 
     for u in range(2):
         src_ref = z_ref if u == 0 else out_ref
         if u == 1:
+            spread_weights(u)
             normalize(src_ref, u)
             for s in range(slots):
                 for off in others:
@@ -209,33 +240,24 @@
         hidden = w_out.shape[1]
         slots = hidden // n
         full = npx * rows
-        updates = w_in.shape[0]
-        zero = jnp.zeros((), BF16)
-        eye8 = jnp.eye(SUB, dtype=jnp.bool_)
-        eye4 = jnp.eye(GATE_ROWS, dtype=jnp.bool_)
-
-        w_t = jnp.swapaxes(w_in, 1, 2)
-        wab = w_t[:, :4 * hidden].reshape(updates, 4, slots, n, dim).transpose(0, 2, 1, 3, 4)
-        wab = wab.reshape(updates, slots, 4 * n, 1, 1, dim)
-        wab = jnp.where(eye8[:, :, None], wab, zero).reshape(updates, slots, 4 * n * SUB, SUB * dim)
-        bab = b_in[:, :4 * hidden].astype(F32).reshape(updates, 4, slots, n).transpose(0, 2, 1, 3)
-        wg = w_t[:, 4 * hidden:].reshape(updates, 1, dim, 1, dim)
-        wg = jnp.where(eye4[:, None, :, None], wg, zero).reshape(updates, GATE_ROWS * dim, GATE_ROWS * dim)
-        wo = jnp.swapaxes(w_out, 1, 2).reshape(updates, 1, dim, hidden, 1)
-        wo = jnp.where(eye8[:, None, None, :], wo, zero).reshape(updates, SUB * dim, SUB * hidden)
-        bg = jnp.broadcast_to(b_in[:, 4 * hidden:, None].astype(F32), (updates, dim, 128))
-        bo = jnp.broadcast_to(b_out[:, :, None].astype(F32), (updates, dim, 128))
-        ln_i = jnp.broadcast_to(ln_in[:, :, :, None].astype(F32), (updates, 2, dim, 128))
-        ln_o = jnp.broadcast_to(ln_out[:, :, :, None, None].astype(F32), (updates, 2, hidden, SUB, 128))
+        width = w_in.shape[2]
+        gate_at = 4 * hidden
+        vec = jnp.concatenate([ln_in, b_in[:, None, gate_at:], b_out[:, None], ln_out], axis=1)
+        vec = jnp.broadcast_to(vec.astype(F32)[..., None], (*vec.shape, 128))
+        bias = b_in.astype(F32)
 
         vmem = pl.BlockSpec(memory_space=pltpu.VMEM)
         smem = pl.BlockSpec(memory_space=pltpu.SMEM)
         out = pl.pallas_call(
             functools.partial(kernel, npy, npx),
             out_shape=jax.ShapeDtypeStruct((rows, dim, cols), BF16),
-            in_specs=[vmem, vmem, vmem, smem] + [vmem] * 6,
+            in_specs=[vmem, vmem, vmem, vmem, smem, vmem],
             out_specs=vmem,
             scratch_shapes=[
+                pltpu.VMEM((width, SUB * dim), BF16),
+                pltpu.VMEM((slots, 4 * n * SUB, SUB * dim), BF16),
+                pltpu.VMEM((GATE_ROWS * dim, GATE_ROWS * dim), BF16),
+                pltpu.VMEM((SUB * dim, SUB * hidden), BF16),
                 pltpu.VMEM((rows, dim, cols), BF16),
                 pltpu.VMEM((2, SUB * max(4 * n, dim), cols), F32),
                 pltpu.VMEM((SUB * hidden, cols), BF16),
@@ -252,7 +274,7 @@
             ],
             compiler_params=pltpu.CompilerParams(collective_id=0, has_side_effects=True, vmem_limit_bytes=67043328),
             name='triangle',
-        )(jnp.swapaxes(pair_blk, 1, 2), mask_blk, wab, bab, ln_i, wg, bg, ln_o, wo, bo)
+        )(jnp.swapaxes(pair_blk, 1, 2), mask_blk, w_in, w_out, bias, vec)
         return jnp.swapaxes(out, 1, 2)
 
     return jax.shard_map(device_body, mesh=mesh, in_specs=(pair_spec, mask_spec, whole, whole, whole, whole, whole, whole), out_specs=pair_spec, check_vma=False)

time: 571 us -> 571 us (level)
  the two profiles are of different devices: /device:TPU:104 before, /device:TPU:97 now
where the time goes in v2:
time: 571 us; the launch traced here: 570 us
  Pallas kernels  561 us (98%)
  local copies, waits for them, and re-layouts  7.02 us (1%)
    pallas_call x1, Pallas kernels, device_body(): pl.pallas_call(functools.partial(kernel, npy, npx), out_shape=jax.ShapeDt...  561 us

profile of v2, /device:TPU:97, one launch (start us, length us, event | category | flops | bytes accessed | tf_op | source)
XLA Modules:
  0.0 570.3 jit_solution(6305316964254057154)
XLA Ops:
  0.0 0.7 slice_bitcast_fusion
  0.7 0.7 copy.10
  1.3 1.3 convert_element_type.10.bias_ref
  2.6 0.7 maximum_convert_fusion
  3.3 0.9 broadcast_in_dim.2.vec_ref
  4.2 561.3 %triangle.1 = bf16[128,64,256]{2,1,0:T(8,128)(2,1)} custom-call(bf16[128,64,256]{2,1,0:T(8,128)(2,1)} %bitcast.6, s32[128,256]{1,0:T(8,128)} %mask_ref.1, bf16[2,64,320]{2,1,0:T(8,128)(2,1)} %w_in_ref.1, bf16[2,64,64]{2,1,0:T(8,128)(2,1)} %w_out_ref.1, f32[2,320]{1,0:T(2,128)} %convert_element_type.10.bias_ref, f32[2,6,64,128]{3,2,1,0:T(8,128)} %broadcast_in_dim.2.vec_ref), custom_call_target="tpu_custom_call" | custom-call | tf_op jit(solution)/shard_map/triangle/pallas_call | solution.py:251
  565.6 4.8 copy.12
  (1 shorter events, 0.0 us)

commit v3 on v2

--- a/solution.py
+++ b/solution.py
@@ -27,7 +27,7 @@
 
 def kernel(npy, npx, z_ref, mask_ref, w_in_ref, w_out_ref, bias_ref, vec_ref,
            out_ref, w_t, wab, wg, wo, zn, proj, xn, ab_out, ab_in, a_t, x_out, x_in,
-           ab_ss, ab_rs, x_ss, x_rs, free_sem):
+           ab_hop, x_hop, ab_ss, ab_rs, x_ss, x_rs, ab_hr, ab_fs, x_hr, x_fs, free_sem):
     rows, dim, cols = z_ref.shape
     hidden = x_in.shape[0]
     width = w_in_ref.shape[2]
@@ -53,13 +53,32 @@
 
     me = (my_py, my_px)
     here = lin(me)
-    def reach(off):
-        hops = [min(off[0], npy - off[0]), min(off[1], nx - off[1])]
-        halfway = 2 * off[0] == npy or 2 * off[1] == nx
-        return halfway, sum(hops)
+    def halfway(off):
+        return (npy > 2 and 2 * off[0] == npy) or (nx > 2 and 2 * off[1] == nx)
 
     diagonal = [((k + k // nx) % npy, k % nx, e) for k in range(npy * nx) for e in range(2)]
-    others = sorted([off for off in diagonal if off != (0, 0, 0)], key=reach)
+    others = [off for off in diagonal if off != (0, 0, 0)]
+    near = [off for off in others if not halfway(off)]
+    far = [off for off in others if halfway(off)]
+
+    def legs(s, off):
+        f, t, e = off
+        turn = 1 if (s + e) % 2 == 0 else -1
+        f1 = turn % npy if npy > 2 and 2 * f == npy else f
+        t1 = turn % nx if nx > 2 and 2 * t == nx else t
+        return (f1, t1, e), ((f - f1) % npy, (t - t1) % nx, 0)
+
+    def each_other(body):
+        @pl.loop(1, n)
+        def _(k):
+            dev = lax.rem(here + k, n)
+            body((dev // npx, lax.rem(dev, npx)))
+
+    def signal_all(sem):
+        each_other(lambda dev: pl.semaphore_signal(sem, inc=1, device_id=dev_id(dev), device_id_type=MESH))
+
+    def back(off):
+        return (-off[0]) % npy, (-off[1]) % nx, off[2]
 
     def at_rows(dev):
         return pl.ds(pl.multiple_of(dev[1] * rows, rows), rows)
@@ -78,6 +97,40 @@
             src_ref=x_out.at[s, at_rows(dst), at_cols(dst)], dst_ref=x_in.at[s * n + lin(src)],
             send_sem=x_ss.at[s, lin(dst)], recv_sem=x_rs.at[s, lin(src)],
             device_id=dev_id(dst), device_id_type=MESH)
+
+    def remote(src, dst, send_sem, recv_sem, dev):
+        return pltpu.make_async_remote_copy(src_ref=src, dst_ref=dst, send_sem=send_sem, recv_sem=recv_sem,
+                                            device_id=dev_id(dev), device_id_type=MESH)
+
+    def ab_first(s, k):
+        return remote(ab_out.at[s, lin(peer(far[k]))], ab_hop.at[s, k], ab_ss.at[s, lin(peer(far[k]))], ab_hr.at[s, k],
+                      peer(legs(s, far[k])[0]))
+
+    def ab_second(s, k):
+        first, second = legs(s, far[k])
+        src = peer(back(first))
+        return remote(ab_hop.at[s, k], ab_in.at[s, :, at_rows(src), at_cols(src)], ab_fs.at[s, k], ab_rs.at[s, lin(src)], peer(second))
+
+    def x_first(s, k):
+        dst = peer(far[k])
+        return remote(x_out.at[s, at_rows(dst), at_cols(dst)], x_hop.at[s, k], x_ss.at[s, lin(dst)], x_hr.at[s, k],
+                      peer(legs(s, far[k])[0]))
+
+    def x_second(s, k):
+        first, second = legs(s, far[k])
+        src = peer(back(first))
+        return remote(x_hop.at[s, k], x_in.at[s * n + lin(src)], x_fs.at[s, k], x_rs.at[s, lin(src)], peer(second))
+
+    def ab_left(s, k):
+        return remote(ab_hop.at[s, k], ab_in.at[s, :, at_rows(me), at_cols(me)], ab_fs.at[s, k], ab_rs.at[s, here], me)
+
+    def x_left(s, k):
+        return remote(x_hop.at[s, k], x_in.at[s * n + here], x_fs.at[s, k], x_rs.at[s, here], me)
+
+    def pass_on(first, second, s):
+        for k in range(len(far)):
+            first(s, k).wait_recv()
+            second(s, k).start()
 
     def iota(shape, axis):
         return lax.broadcasted_iota(jnp.int32, shape, axis)
@@ -137,7 +190,9 @@
                     ab_out[s, d, op, at, :] = (mask * jax.nn.sigmoid(gate) * lin_p).astype(BF16)
 
     def send_ab(s):
-        for off in others:
+        for k in range(len(far)):
+            ab_first(s, k).start()
+        for off in near:
             ab_copy(s, me, peer(off)).start()
         ab_in[s, :, at_rows(me), at_cols(me)] = ab_out[s, here]
 
@@ -159,7 +214,9 @@
                 else:
                     x_out[s, m_at, q_at] = dot(lhs_ref[...], ab_in[s, 1, :, q_at])
 
-        for off in others:
+        for k in range(len(far)):
+            x_first(s, k).start()
+        for off in near:
             x_copy(s, me, peer(off)).start()
         x_in[s * n + here] = x_out[s, at_rows(me), at_cols(me)]
 
@@ -190,11 +247,16 @@
                     out_ref[g * SUB + r, :, lanes] = (src_ref[g * SUB + r, :, lanes].astype(F32) + gate * upd).astype(BF16)
 
     barrier = pltpu.get_barrier_semaphore()
-    for off in others:
-        pl.semaphore_signal(barrier, inc=1, device_id=dev_id(peer(off)), device_id_type=MESH)
+    signal_all(barrier)
     spread_weights(0)
     normalize(z_ref, 0)
     pl.semaphore_wait(barrier, n - 1)
+
+    def wait_forwards(second):
+        for s in range(slots):
+            @pl.loop(0, len(far))
+            def _(k):
+                second(s, k).wait_send()
 
     for u in range(2):
         src_ref = z_ref if u == 0 else out_ref
@@ -202,30 +264,30 @@
             spread_weights(u)
             normalize(src_ref, u)
             for s in range(slots):
-                for off in others:
-                    ab_copy(s, me, peer(off)).wait_send()
+                each_other(lambda dev: ab_copy(s, me, dev).wait_send())
+            wait_forwards(x_left)
             pl.semaphore_wait(free_sem, n - 1)
         for s in range(slots):
             project(u, s)
             send_ab(s)
         for s in range(slots):
-            for off in others:
-                ab_copy(s, peer(off), me).wait_recv()
+            pass_on(ab_first, ab_second, s)
+            each_other(lambda dev: ab_copy(s, dev, me).wait_recv())
             if u == 1:
-                for off in others:
-                    x_copy(s, me, peer(off)).wait_send()
+                each_other(lambda dev: x_copy(s, me, dev).wait_send())
             products(u, s)
+        wait_forwards(ab_left)
         if u == 0:
-            for off in others:
-                pl.semaphore_signal(free_sem, inc=1, device_id=dev_id(peer(off)), device_id_type=MESH)
-        for s in range(slots):
-            for off in others:
-                x_copy(s, peer(off), me).wait_recv()
+            signal_all(free_sem)
+        for s in range(slots):
+            pass_on(x_first, x_second, s)
+        for s in range(slots):
+            each_other(lambda dev: x_copy(s, dev, me).wait_recv())
         finish(src_ref, u)
     for s in range(slots):
-        for off in others:
-            ab_copy(s, me, peer(off)).wait_send()
-            x_copy(s, me, peer(off)).wait_send()
+        each_other(lambda dev: ab_copy(s, me, dev).wait_send())
+        each_other(lambda dev: x_copy(s, me, dev).wait_send())
+    wait_forwards(x_left)
 
 
 def solution(mesh):
@@ -240,6 +302,8 @@
         hidden = w_out.shape[1]
         slots = hidden // n
         full = npx * rows
+        nx = npx // 2
+        n_far = max(1, n - (npy - (npy > 2)) * (nx - (nx > 2)) * 2)
         width = w_in.shape[2]
         gate_at = 4 * hidden
         vec = jnp.concatenate([ln_in, b_in[:, None, gate_at:], b_out[:, None], ln_out], axis=1)
@@ -266,10 +330,10 @@
                 pltpu.VMEM((2 * rows, full), BF16),
                 pltpu.VMEM((slots, full, full), F32),
                 pltpu.VMEM((hidden, rows, cols), F32),
-                pltpu.SemaphoreType.DMA((slots, n)),
-                pltpu.SemaphoreType.DMA((slots, n)),
-                pltpu.SemaphoreType.DMA((slots, n)),
-                pltpu.SemaphoreType.DMA((slots, n)),
+                pltpu.VMEM((slots, n_far, 2, rows, cols), BF16),
+                pltpu.VMEM((slots, n_far, rows, cols), F32),
+                *[pltpu.SemaphoreType.DMA((slots, n))] * 4,
+                *[pltpu.SemaphoreType.DMA((slots, n_far))] * 4,
                 pltpu.SemaphoreType.REGULAR,
             ],
             compiler_params=pltpu.CompilerParams(collective_id=0, has_side_effects=True, vmem_limit_bytes=67043328),

time: 571 us -> 496 us (0.87)
  the two profiles are of different devices: /device:TPU:97 before, /device:TPU:98 now
where the time goes in v3:
time: 496 us; the launch traced here: 495 us
  Pallas kernels  486 us (98%)
  local copies, waits for them, and re-layouts  7.02 us (1%)
    pallas_call x1, Pallas kernels, device_body(): pl.pallas_call(functools.partial(kernel, npy, npx), out_shape=jax.ShapeDt...  486 us

profile of v3, /device:TPU:98, one launch (start us, length us, event | category | flops | bytes accessed | tf_op | source)
XLA Modules:
  0.0 495.4 jit_solution(10038510403740982391)
XLA Ops:
  0.0 0.7 slice_bitcast_fusion
  0.7 0.7 copy.10
  1.3 1.3 convert_element_type.10.bias_ref
  2.6 0.7 maximum_convert_fusion
  3.3 0.9 broadcast_in_dim.2.vec_ref
  4.2 486.3 %triangle.1 = bf16[128,64,256]{2,1,0:T(8,128)(2,1)} custom-call(bf16[128,64,256]{2,1,0:T(8,128)(2,1)} %bitcast.6, s32[128,256]{1,0:T(8,128)} %mask_ref.1, bf16[2,64,320]{2,1,0:T(8,128)(2,1)} %w_in_ref.1, bf16[2,64,64]{2,1,0:T(8,128)(2,1)} %w_out_ref.1, f32[2,320]{1,0:T(2,128)} %convert_element_type.10.bias_ref, f32[2,6,64,128]{3,2,1,0:T(8,128)} %broadcast_in_dim.2.vec_ref), custom_call_target="tpu_custom_call" | custom-call | tf_op jit(solution)/shard_map/triangle/pallas_call | solution.py:315
  490.6 4.8 copy.12
  (1 shorter events, 0.0 us)

commit v4 on v2

v4 whole, which is shorter than its diff:
```python
import functools

import jax
import jax.numpy as jnp
from jax import lax
from jax.experimental import pallas as pl
from jax.experimental.pallas import tpu as pltpu
from jax.sharding import PartitionSpec as P

LN_EPS = 1e-5
SUB = 8
GATE_ROWS = 4
MESH = pl.DeviceIdType.MESH
BF16 = jnp.bfloat16
F32 = jnp.float32


def dot(lhs, rhs, dims=((1,), (0,))):
    return lax.dot_general(lhs, rhs, (dims, ((), ())), preferred_element_type=F32)


def tree_sum(parts):
    while len(parts) > 1:
        parts = [parts[k] + parts[k + 1] if k + 1 < len(parts) else parts[k] for k in range(0, len(parts), 2)]
    return parts[0]


def kernel(npy, npx, z_ref, mask_ref, w_in_ref, w_out_ref, vec_ref,
           out_ref, w_t, wab, wg, wo, zn, proj, xn, ab_out, ab_in, a_t, x_out, x_in,
           ab_hop, x_hop, ab_ss, ab_rs, x_ss, x_rs, ab_hr, ab_fs, x_hr, x_fs, free_sem):
    rows, dim, cols = z_ref.shape
    hidden = x_in.shape[0]
    width = w_in_ref.shape[2]
    n = npy * npx
    slots = hidden // n
    full = npx * rows
    tile = 2 * rows
    my_py, my_px = lax.axis_index('py'), lax.axis_index('px')
    my_x, my_core = my_px // 2, lax.rem(my_px, 2)
    nx = npx // 2

    def peer(off):
        f, t, e = off
        dpy = lax.rem(my_py + f, npy)
        dpx = 2 * lax.rem(my_x + t, nx) + lax.rem(my_core + e, 2)
        return dpy, dpx

    def lin(dev):
        return dev[0] * npx + dev[1]

    def dev_id(dev):
        return {'py': dev[0], 'px': dev[1]}

    me = (my_py, my_px)
    here = lin(me)
    ring_y, ring_x = npy > 2 and npy % 2 == 0, nx > 2 and nx % 2 == 0
    num_y, num_x = npy - ring_y, nx - ring_x
    num_far = 2 * (npy * nx - num_y * num_x)

    half = rows // 2
    ab_parts = [(0, 0, half), (0, half, half)] + [(s, 0, rows) for s in range(1, slots)]
    last = slots
    x_parts = [(s, 0, rows) for s in range(slots - 1)] + [(slots - 1, 0, half), (slots - 1, half, half)]

    def straight(k, size, ring):
        return k + lax.div(k, size // 2) if ring else k

    def each_near(body):
        @pl.loop(1, 2 * num_y * num_x)
        def _(k):
            step = lax.div(k, 2)
            f = straight(lax.rem(step + lax.div(step, num_x), num_y), npy, ring_y)
            t = straight(lax.rem(step, num_x), nx, ring_x)
            body(peer((f, t, lax.rem(k, 2))))

    def each_far(p, body):
        def visit(k, f, t, e, over_y, over_x):
            turn = 1 - 2 * lax.rem(p + e, 2)
            f1 = lax.rem(turn + npy, npy) if over_y else f
            t1 = lax.rem(turn + nx, nx) if over_x else t
            f2, t2 = lax.rem(f - f1 + npy, npy), lax.rem(t - t1 + nx, nx)
            origin = peer((lax.rem(npy - f1, npy), lax.rem(nx - t1, nx), e))
            body(k, peer((f, t, e)), peer((f1, t1, e)), origin, peer((f2, t2, 0)))

        if ring_x:
            @pl.loop(0, 2 * num_y)
            def _(k):
                visit(k, straight(lax.div(k, 2), npy, ring_y), nx // 2, lax.rem(k, 2), False, True)
        if ring_y:
            @pl.loop(0, 2 * num_x)
            def _(k):
                visit(2 * num_y * ring_x + k, npy // 2, straight(lax.div(k, 2), nx, ring_x), lax.rem(k, 2), True, False)
        if ring_x and ring_y:
            @pl.loop(0, 2)
            def _(k):
                visit(2 * (num_y + num_x) + k, npy // 2, nx // 2, k, True, True)

    def each_other(body):
        @pl.loop(1, n)
        def _(k):
            dev = lax.rem(here + k, n)
            body((dev // npx, lax.rem(dev, npx)))

    def signal_all(sem):
        each_other(lambda dev: pl.semaphore_signal(sem, inc=1, device_id=dev_id(dev), device_id_type=MESH))

    def at_rows(dev, first=0, count=rows):
        return pl.ds(pl.multiple_of(dev[1] * rows + first, count), count)

    def at_cols(dev):
        return pl.ds(pl.multiple_of(dev[0] * cols, cols), cols)

    def remote(src, dst, send_sem, recv_sem, dev):
        return pltpu.make_async_remote_copy(src_ref=src, dst_ref=dst, send_sem=send_sem, recv_sem=recv_sem,
                                            device_id=dev_id(dev), device_id_type=MESH)

    def ab_place(p, src):
        s, first, count = ab_parts[p]
        return ab_in.at[s, :, at_rows(src, first, count), at_cols(src)]

    def ab_from(p, dst):
        s, first, count = ab_parts[p]
        return ab_out.at[s, lin(dst), :, pl.ds(first, count), :]

    def ab_stop(p, k):
        s, first, count = ab_parts[p]
        return ab_hop.at[s, k, :, pl.ds(first, count), :]

    def x_place(p, src):
        s, first, count = x_parts[p]
        return x_in.at[s * n + lin(src), pl.ds(first, count), :]

    def x_from(p, dst):
        s, first, count = x_parts[p]
        return x_out.at[s, at_rows(dst, first, count), at_cols(dst)]

    def x_stop(p, k):
        s, first, count = x_parts[p]
        return x_hop.at[s, k, pl.ds(first, count), :]

    def ab_copy(p, src, dst):
        return remote(ab_from(p, dst), ab_place(p, src), ab_ss.at[p, lin(dst)], ab_rs.at[p, lin(src)], dst)

    def x_copy(p, src, dst):
        return remote(x_from(p, dst), x_place(p, src), x_ss.at[p, lin(dst)], x_rs.at[p, lin(src)], dst)

    def ab_first(p, k, dst, stop):
        return remote(ab_from(p, dst), ab_stop(p, k), ab_ss.at[p, lin(dst)], ab_hr.at[p, k], stop)

    def ab_second(p, k, origin, dst):
        return remote(ab_stop(p, k), ab_place(p, origin), ab_fs.at[p, k], ab_rs.at[p, lin(origin)], dst)

    def x_first(p, k, dst, stop):
        return remote(x_from(p, dst), x_stop(p, k), x_ss.at[p, lin(dst)], x_hr.at[p, k], stop)

    def x_second(p, k, origin, dst):
        return remote(x_stop(p, k), x_place(p, origin), x_fs.at[p, k], x_rs.at[p, lin(origin)], dst)

    def ab_left(p, k):
        return remote(ab_stop(p, k), ab_place(p, me), ab_fs.at[p, k], ab_rs.at[p, here], me)

    def x_left(p, k):
        return remote(x_stop(p, k), x_place(p, me), x_fs.at[p, k], x_rs.at[p, here], me)

    def pass_on(first, second, p):
        def body(k, dst, stop, origin, onward):
            first(p, k, dst, stop).wait_recv()
            second(p, k, origin, onward).start()
        each_far(p, body)

    def send(first, copy, p):
        each_far(p, lambda k, dst, stop, origin, onward: first(p, k, dst, stop).start())
        each_near(lambda dev: copy(p, me, dev).start())

    def wait_forwards(left, parts):
        for p in parts:
            @pl.loop(0, num_far)
            def _(k):
                left(p, k).wait_send()

    def wait_sent(copy, parts):
        for p in range(len(parts)):
            each_other(lambda dev: copy(p, me, dev).wait_send())

    def iota(shape, axis):
        return lax.broadcasted_iota(jnp.int32, shape, axis)

    def spread_in(u):
        wide = (dim, SUB * dim)
        pick = (lax.rem(iota(wide, 1), dim) == iota(wide, 0)).astype(F32).astype(BF16)
        w_t[...] = dot(w_in_ref[u], pick, ((0,), (0,))).astype(BF16)
        big = (n * SUB, SUB * dim)
        keep = lax.rem(iota(big, 0), SUB) == iota(big, 1) // dim
        sel = (n * SUB, width)
        for s in range(slots):
            for k in range(4):
                first = k * hidden + s * n
                rep = (iota(sel, 0) // SUB + first == iota(sel, 1)).astype(F32).astype(BF16)
                wab[s, pl.ds(k * n * SUB, n * SUB), :] = jnp.where(keep, dot(rep, w_t[...]), 0.0).astype(BF16)

    def spread_out(u):
        gate_w = w_t[pl.ds(4 * hidden, dim), pl.ds(0, GATE_ROWS * dim)].astype(F32)
        lane = iota(gate_w.shape, 1)
        for r in range(GATE_ROWS):
            wg[pl.ds(r * dim, dim), :] = jnp.where(lane // dim == r, gate_w, 0.0).astype(BF16)
        wide = (hidden, SUB * hidden)
        pick = (iota(wide, 1) // SUB == iota(wide, 0)).astype(F32).astype(BF16)
        out_w = dot(w_out_ref[u], pick, ((0,), (0,)))
        lane = iota(out_w.shape, 1)
        for r in range(SUB):
            wo[pl.ds(r * dim, dim), :] = jnp.where(lax.rem(lane, SUB) == r, out_w, 0.0).astype(BF16)

    def normalize(src_ref, u, start, count):
        gain, shift = vec_ref[u, 0], vec_ref[u, 1]

        @pl.loop(start, start + count, unroll=4)
        def _(i):
            for h in range(cols // 128):
                lanes = pl.ds(h * 128, 128)
                val = src_ref[i, :, lanes].astype(F32)
                cen = val - jnp.mean(val, axis=0, keepdims=True)
                var = jnp.mean(cen * cen, axis=0, keepdims=True)
                zn[i, :, lanes] = (cen * lax.rsqrt(var + LN_EPS) * gain + shift).astype(BF16)

    def project(u, p):
        s, start, count = ab_parts[p]

        @pl.loop(start // (2 * SUB), (start + count) // (2 * SUB))
        def _(g):
            for h in range(2):
                rhs = zn[pl.ds(g * 2 * SUB + h * SUB, SUB)].reshape(SUB * dim, cols)
                proj[h, pl.ds(0, 4 * n * SUB), :] = dot(wab[s], rhs)
            at = pl.ds(pl.multiple_of(g * 2 * SUB, 2 * SUB), 2 * SUB)
            mask = mask_ref[at, :].astype(F32)

            @pl.loop(0, n, unroll=4)
            def _(d):
                for op in range(2):
                    bias_g, bias_p = [jnp.concatenate([vec_ref[u, 2 + 2 * op + k, pl.ds(s * n + d, 1), :]] * (cols // 128), axis=1) for k in range(2)]
                    g_at = pl.ds(pl.multiple_of((2 * op * n + d) * SUB, SUB), SUB)
                    p_at = pl.ds(pl.multiple_of(((2 * op + 1) * n + d) * SUB, SUB), SUB)
                    gate = jnp.concatenate([proj[0, g_at, :], proj[1, g_at, :]], axis=0) + bias_g
                    lin_p = jnp.concatenate([proj[0, p_at, :], proj[1, p_at, :]], axis=0) + bias_p
                    ab_out[s, d, op, at, :] = (mask * jax.nn.sigmoid(gate) * lin_p).astype(BF16)

    def send_ab(p):
        s, start, count = ab_parts[p]
        send(ab_first, ab_copy, p)
        ab_in[s, :, at_rows(me, start, count), at_cols(me)] = ab_out[s, here, :, pl.ds(start, count), :]

    def products(u, s):
        for t in range(nx):
            m = lax.rem(my_x + t, nx)
            m_at = pl.ds(pl.multiple_of(m * tile, tile), tile)
            if u == 0:
                lhs_ref = ab_in.at[s, 0, m_at, :]
            else:
                a_t[...] = ab_in[s, 0, :, m_at].T
                lhs_ref = a_t

            @pl.loop(0, full // cols)
            def _(q):
                q_at = pl.ds(pl.multiple_of(q * cols, cols), cols)
                if u == 0:
                    x_out[s, m_at, q_at] = dot(lhs_ref[...], ab_in[s, 1, q_at, :], ((1,), (1,)))
                else:
                    x_out[s, m_at, q_at] = dot(lhs_ref[...], ab_in[s, 1, :, q_at])

        for p, part in enumerate(x_parts):
            if part[0] == s and p < last:
                send(x_first, x_copy, p)
        x_in[s * n + here] = x_out[s, at_rows(me), at_cols(me)]

    def finish(src_ref, u, start, count):
        @pl.loop(start // SUB, (start + count) // SUB)
        def _(g):
            at = pl.ds(pl.multiple_of(g * SUB, SUB), SUB)
            for h in range(cols // 128):
                lanes = pl.ds(h * 128, 128)
                avg = tree_sum([x_in[c, at, lanes] for c in range(hidden)]) * (1.0 / hidden)
                var = tree_sum([jnp.square(x_in[c, at, lanes] - avg) for c in range(hidden)]) * (1.0 / hidden)
                inv = lax.rsqrt(var + LN_EPS)
                for c in range(0, hidden, 2):
                    pair = [(x_in[k, at, lanes] - avg) * inv * vec_ref[u, 8, pl.ds(k, 1), :] + vec_ref[u, 9, pl.ds(k, 1), :] for k in (c, c + 1)]
                    xn[pl.ds(c * SUB, 2 * SUB), lanes] = jnp.concatenate(pair, axis=0).astype(BF16)
            proj[0, pl.ds(0, SUB * dim), :] = dot(wo[...], xn[...])
            for k in range(SUB // GATE_ROWS):
                rhs = zn[pl.ds(g * SUB + k * GATE_ROWS, GATE_ROWS)].reshape(GATE_ROWS * dim, cols)
                proj[1, pl.ds(k * GATE_ROWS * dim, GATE_ROWS * dim), :] = dot(wg[...], rhs)

            @pl.loop(0, SUB, unroll=4)
            def _(r):
                r_at = pl.ds(pl.multiple_of(r * dim, dim), dim)
                for h in range(cols // 128):
                    lanes = pl.ds(h * 128, 128)
                    gate = jax.nn.sigmoid(proj[1, r_at, lanes] + vec_ref[u, 6])
                    upd = proj[0, r_at, lanes] + vec_ref[u, 7]
                    out_ref[g * SUB + r, :, lanes] = (src_ref[g * SUB + r, :, lanes].astype(F32) + gate * upd).astype(BF16)

    barrier = pltpu.get_barrier_semaphore()
    signal_all(barrier)
    early_x, last_x = list(range(slots - 1)), [last - 1, last]

    def begin(src_ref, u, h):
        normalize(src_ref, u, h * half, half)
        project(u, h)

    spread_in(0)
    begin(z_ref, 0, 0)
    pl.semaphore_wait(barrier, n - 1)
    for u in range(2):
        src_ref = z_ref if u == 0 else out_ref
        if u == 0:
            send_ab(0)
            begin(src_ref, u, 1)
            send_ab(1)
        for p in range(2, len(ab_parts)):
            project(u, p)
            if u == 1 and p == len(ab_parts) - 1:
                wait_forwards(x_left, last_x)
            send_ab(p)
        spread_out(u)
        if u == 1:
            wait_sent(x_copy, x_parts)
        for s in range(slots):
            for p, part in enumerate(ab_parts):
                if part[0] == s:
                    pass_on(ab_first, ab_second, p)
            for p, part in enumerate(ab_parts):
                if part[0] == s:
                    each_other(lambda dev: ab_copy(p, dev, me).wait_recv())
            products(u, s)
        wait_forwards(ab_left, range(len(ab_parts)))
        wait_sent(ab_copy, ab_parts)
        if u == 0:
            signal_all(free_sem)
            spread_in(1)
        for p in range(last):
            pass_on(x_first, x_second, p)
        send(x_first, x_copy, last)
        for p in range(last):
            each_other(lambda dev: x_copy(p, dev, me).wait_recv())
        finish(src_ref, u, 0, half)
        pass_on(x_first, x_second, last)
        if u == 0:
            begin(out_ref, 1, 0)
            pl.semaphore_wait(free_sem, n - 1)
            send_ab(0)
        each_other(lambda dev: x_copy(last, dev, me).wait_recv())
        finish(src_ref, u, half, half)
        if u == 0:
            begin(out_ref, 1, 1)
            wait_forwards(x_left, early_x if slots > 1 else last_x)
            send_ab(1)
    wait_sent(x_copy, x_parts)
    wait_forwards(x_left, early_x + last_x)


def solution(mesh):
    pair_spec = P(('batch', 'px'), 'py', None)
    mask_spec = P(('batch', 'px'), 'py')
    whole = P()
    npy, npx = mesh.shape['py'], mesh.shape['px']
    n = npy * npx

    def device_body(pair_blk, mask_blk, ln_in, w_in, b_in, ln_out, w_out, b_out):
        rows, cols, dim = pair_blk.shape
        hidden = w_out.shape[1]
        slots = hidden // n
        full = npx * rows
        nx = npx // 2
        n_far = max(1, n - (npy - (npy > 2)) * (nx - (nx > 2)) * 2)
        width = w_in.shape[2]
        vec = jnp.concatenate([ln_in, b_in.reshape(b_in.shape[0], -1, dim), b_out[:, None], ln_out], axis=1)
        vec = jnp.broadcast_to(vec.astype(F32)[..., None], (*vec.shape, 128))

        vmem = pl.BlockSpec(memory_space=pltpu.VMEM)
        out = pl.pallas_call(
            functools.partial(kernel, npy, npx),
            out_shape=jax.ShapeDtypeStruct((rows, dim, cols), BF16),
            in_specs=[vmem] * 5,
            out_specs=vmem,
            scratch_shapes=[
                pltpu.VMEM((width, SUB * dim), BF16),
                pltpu.VMEM((slots, 4 * n * SUB, SUB * dim), BF16),
                pltpu.VMEM((GATE_ROWS * dim, GATE_ROWS * dim), BF16),
                pltpu.VMEM((SUB * dim, SUB * hidden), BF16),
                pltpu.VMEM((rows, dim, cols), BF16),
                pltpu.VMEM((2, SUB * max(4 * n, dim), cols), F32),
                pltpu.VMEM((SUB * hidden, cols), BF16),
                pltpu.VMEM((slots, n, 2, rows, cols), BF16),
                pltpu.VMEM((slots, 2, full, full), BF16),
                pltpu.VMEM((2 * rows, full), BF16),
                pltpu.VMEM((slots, full, full), F32),
                pltpu.VMEM((hidden, rows, cols), F32),
                pltpu.VMEM((slots, n_far, 2, rows, cols), BF16),
                pltpu.VMEM((slots, n_far, rows, cols), F32),
                *[pltpu.SemaphoreType.DMA((slots + 1, n))] * 4,
                *[pltpu.SemaphoreType.DMA((slots + 1, n_far))] * 4,
                pltpu.SemaphoreType.REGULAR,
            ],
            compiler_params=pltpu.CompilerParams(collective_id=0, has_side_effects=True, vmem_limit_bytes=67043328),
            name='triangle',
        )(jnp.swapaxes(pair_blk, 1, 2), mask_blk, w_in, w_out, vec)
        return jnp.swapaxes(out, 1, 2)

    return jax.shard_map(device_body, mesh=mesh, in_specs=(pair_spec, mask_spec, whole, whole, whole, whole, whole, whole), out_specs=pair_spec, check_vma=False)
```

time: 571 us -> 457 us (0.80)
  the two profiles are of different devices: /device:TPU:97 before, /device:TPU:98 now
where the time goes in v4:
time: 457 us; the launch traced here: 455 us
  Pallas kernels  447 us (98%)
  local copies, waits for them, and re-layouts  7.28 us (2%)
    pallas_call x1, Pallas kernels, device_body(): pl.pallas_call(functools.partial(kernel, npy, npx), out_shape=jax.ShapeDt...  447 us

profile of v4, /device:TPU:98, one launch (start us, length us, event | category | flops | bytes accessed | tf_op | source)
XLA Modules:
  0.0 455.3 jit_solution(1131490060896942866)
XLA Ops:
  0.0 0.7 copy.10
  0.7 0.8 concatenate.11
  1.4 0.7 maximum_convert_fusion
  2.1 1.1 broadcast_in_dim.2.vec_ref
  3.2 447.3 %triangle.1 = bf16[128,64,256]{2,1,0:T(8,128)(2,1)} custom-call(bf16[128,64,256]{2,1,0:T(8,128)(2,1)} %bitcast.4, s32[128,256]{1,0:T(8,128)} %mask_ref.1, bf16[2,64,320]{2,1,0:T(8,128)(2,1)} %w_in_ref.1, bf16[2,64,64]{2,1,0:T(8,128)(2,1)} %w_out_ref.1, f32[2,10,64,128]{3,2,1,0:T(8,128)} %broadcast_in_dim.2.vec_ref), custom_call_target="tpu_custom_call" | custom-call | tf_op jit(solution)/shard_map/triangle/pallas_call | solution.py:378
  450.5 4.8 %copy.12 = bf16[128,256,64]{1,2,0:T(8,128)(2,1)} copy(bf16[128,256,64]{1,2,0:T(8,128)(2,1)} %bitcast.3) | data formatting | bytes 8388608

commit v5 on v4

--- a/solution.py
+++ b/solution.py
@@ -55,7 +55,9 @@
     here = lin(me)
     ring_y, ring_x = npy > 2 and npy % 2 == 0, nx > 2 and nx % 2 == 0
     num_y, num_x = npy - ring_y, nx - ring_x
-    num_far = 2 * (npy * nx - num_y * num_x)
+    halfway = 2 * (npy * nx - num_y * num_x)
+    corners = 4 if ring_x and ring_y else 0
+    num_far = halfway + corners
 
     half = rows // 2
     ab_parts = [(0, 0, half), (0, half, half)] + [(s, 0, rows) for s in range(1, slots)]
@@ -71,16 +73,30 @@
             step = lax.div(k, 2)
             f = straight(lax.rem(step + lax.div(step, num_x), num_y), npy, ring_y)
             t = straight(lax.rem(step, num_x), nx, ring_x)
-            body(peer((f, t, lax.rem(k, 2))))
+            e = lax.rem(k, 2)
+            if corners:
+                is_corner = (e == 1) & ((f == 1) | (f == npy - 1)) & ((t == 1) | (t == nx - 1))
+                pl.when(jnp.logical_not(is_corner))(lambda: body(peer((f, t, e))))
+            else:
+                body(peer((f, t, e)))
 
     def each_far(p, body):
         def visit(k, f, t, e, over_y, over_x):
             turn = 1 - 2 * lax.rem(p + e, 2)
             f1 = lax.rem(turn + npy, npy) if over_y else f
             t1 = lax.rem(turn + nx, nx) if over_x else t
+            stop(k, f, t, e, f1, t1)
+
+        def stop(k, f, t, e, f1, t1):
             f2, t2 = lax.rem(f - f1 + npy, npy), lax.rem(t - t1 + nx, nx)
             origin = peer((lax.rem(npy - f1, npy), lax.rem(nx - t1, nx), e))
             body(k, peer((f, t, e)), peer((f1, t1, e)), origin, peer((f2, t2, 0)))
+
+        if corners:
+            @pl.loop(0, corners)
+            def _(k):
+                f, t = 1 + (npy - 2) * lax.div(k, 2), 1 + (nx - 2) * lax.rem(k, 2)
+                stop(halfway + k, f, t, 1, f, 0)
 
         if ring_x:
             @pl.loop(0, 2 * num_y)
@@ -369,7 +385,7 @@
         slots = hidden // n
         full = npx * rows
         nx = npx // 2
-        n_far = max(1, n - (npy - (npy > 2)) * (nx - (nx > 2)) * 2)
+        n_far = n // 2 + 2 if npy > 2 and nx > 2 else n
         width = w_in.shape[2]
         vec = jnp.concatenate([ln_in, b_in.reshape(b_in.shape[0], -1, dim), b_out[:, None], ln_out], axis=1)
         vec = jnp.broadcast_to(vec.astype(F32)[..., None], (*vec.shape, 128))

time: 457 us -> 449 us (0.982)
  Pallas kernels: 447 us -> 439 us
    pallas_call x1, Pallas kernels: 447 us -> 439 us  [device_body(): pl.pallas_call(functools.partial(kernel, npy, npx), out_shape=jax.ShapeDt...]
where the time goes in v5:
time: 449 us; the launch traced here: 447 us
  Pallas kernels  439 us (98%)
  local copies, waits for them, and re-layouts  7.28 us (2%)
    pallas_call x1, Pallas kernels, device_body(): pl.pallas_call(functools.partial(kernel, npy, npx), out_shape=jax.ShapeDt...  439 us

profile of v5, /device:TPU:98, one launch (start us, length us, event | category | flops | bytes accessed | tf_op | source)
XLA Modules:
  0.0 447.3 jit_solution(3532787918904427575)
XLA Ops:
  0.0 0.7 copy.10
  0.7 0.8 concatenate.11
  1.4 0.7 maximum_convert_fusion
  2.1 1.1 broadcast_in_dim.2.vec_ref
  3.2 439.3 %triangle.1 = bf16[128,64,256]{2,1,0:T(8,128)(2,1)} custom-call(bf16[128,64,256]{2,1,0:T(8,128)(2,1)} %bitcast.4, s32[128,256]{1,0:T(8,128)} %mask_ref.1, bf16[2,64,320]{2,1,0:T(8,128)(2,1)} %w_in_ref.1, bf16[2,64,64]{2,1,0:T(8,128)(2,1)} %w_out_ref.1, f32[2,10,64,128]{3,2,1,0:T(8,128)} %broadcast_in_dim.2.vec_ref), custom_call_target="tpu_custom_call" | custom-call | tf_op jit(solution)/shard_map/triangle/pallas_call | solution.py:394
  442.5 4.8 %copy.12 = bf16[128,256,64]{1,2,0:T(8,128)(2,1)} copy(bf16[128,256,64]{1,2,0:T(8,128)(2,1)} %bitcast.3) | data formatting | bytes 8388608
